TPU v7x, 256 devices: a whole 4x4x8 slice. The times are simulated.
256 devices in a mesh: batch: 4 (over x), heads: 64 (over y, z, core).
Axes of the slice: x: 4, y: 4, z: 8, core: 2. Of those that a mesh axis runs over, the one named last changes fastest.
Arguments:
- draft_ids: int32 [192, 8], P('batch'), may hold values from 0 to 50279
- accepted: int32 [192], P('batch'), may hold values from 1 to 8
- embedding: bfloat16 [50280, 2560], P(None, 'heads'), may hold values from -6 to 6
- norm_gain: float32 [2, 2560], replicated, may hold values from 0.5 to 1.5
- w_zx: bfloat16 [2, 2560, 64, 128], P(None, None, 'heads'), may hold values from -0.125 to 0.125
- w_dt: bfloat16 [2, 2560, 64], P(None, None, 'heads'), may hold values from -0.125 to 0.125
- w_bc: bfloat16 [2, 2560, 256], P(None, None, 'heads'), may hold values from -0.125 to 0.125
- dt_bias: float32 [2, 64], P(None, 'heads'), may hold values from -4 to -1
- decay_rate: float32 [2, 64], P(None, 'heads'), may hold values from 1 to 16
- skip_weight: float32 [2, 64], P(None, 'heads'), may hold values from 0.5 to 1.5
- conv_x_w: bfloat16 [2, 4, 4096], P(None, None, 'heads'), may hold values from -3 to 3
- conv_x_b: bfloat16 [2, 4096], P(None, 'heads'), may hold values from -3 to 3
- conv_bc_w: bfloat16 [2, 4, 256], P(None, None, 'heads'), may hold values from -3 to 3
- conv_bc_b: bfloat16 [2, 256], P(None, 'heads'), may hold values from -3 to 3
- gate_gain: float32 [2, 4096], P(None, 'heads'), may hold values from 0.5 to 1.5
- out_w: bfloat16 [2, 4096, 2560], P(None, 'heads'), may hold values from -0.25 to 0.25
- ssm_state: float32 [2, 192, 64, 64, 128], P(None, 'batch', 'heads'), may hold values from -1.6 to 1.6
- conv_x_state: bfloat16 [2, 192, 3, 4096], P(None, 'batch', None, 'heads'), may hold values from -6 to 6
- conv_bc_state: bfloat16 [2, 192, 3, 256], P(None, 'batch', None, 'heads'), may hold values from -6 to 6
Outputs:
- hidden_out: bfloat16 [1536, 2560], P('batch', 'heads')
- new_ssm: float32 [2, 192, 64, 64, 128], P(None, 'batch', 'heads')
- new_conv_x: bfloat16 [2, 192, 3, 4096], P(None, 'batch', None, 'heads')
- new_conv_bc: bfloat16 [2, 192, 3, 256], P(None, 'batch', None, 'heads')
Inputs may be any that keep to these rules, and one draw needn't show every extreme that they name: `accepted`: the number of a sequence's draft tokens that are kept, counted from the first.
All inputs are finite; a program needn't handle non-finite values.
Results may differ from a plain program's by a relative error of at most 0.015.
Values may be sent and summed in bfloat16 or wider, within the bound.
No kernel may reach another device: no remote copies, remote signals or barrier semaphores. Data moves between devices by JAX's collectives and lax.ppermute only.
A program may use at most 128 MiB of HBM per device.

v0:
```python
import jax
import jax.numpy as jnp
from jax import lax
from jax.sharding import PartitionSpec as P

LAYERS = 2
EPS = 1e-05


def turned_gather(arrays, axis, dims):
    turned = [jnp.moveaxis(a, dim, 0) for a, dim in zip(arrays, dims)]
    widths = [t[0].size for t in turned]
    both = jnp.concatenate([t.reshape(-1, w) for t, w in zip(turned, widths)], axis=1)
    filled = lax.all_gather(both, axis, axis=0, tiled=True)
    blocks = jnp.split(filled, [sum(widths[:k]) for k in range(1, len(widths))], axis=1)
    return tuple(
        (
            jnp.moveaxis(b.reshape(-1, *t.shape[1:]), 0, dim)
            for b, t, dim in zip(blocks, turned, dims)
        )
    )


def in_order(blocks, dim):
    blocks = jnp.moveaxis(blocks, 0, dim)
    dims = blocks.shape
    return blocks.reshape(*dims[:dim], dims[dim] * dims[dim + 1], *dims[dim + 2 :])


def sent_to_all(value, axis):
    count = lax.axis_size(axis)
    return lax.all_to_all(
        jnp.broadcast_to(value[None], (count, *value.shape)), axis, 0, 0, tiled=True
    )


def gather_directly(value, axis, dim):
    return in_order(sent_to_all(value, axis), dim)


def rms_scale(total, count):
    return lax.rsqrt(total / count + EPS)


def convolve(window, weight, bias, count):
    weight = weight.astype(jnp.float32)
    acc = window[:, 0:count] * weight[0]
    for k in range(1, weight.shape[0]):
        acc = acc + window[:, k : k + count] * weight[k]
    return jax.nn.silu(acc + bias.astype(jnp.float32))


def keep_rows(window, accepted, kept_rows):
    last_start = window.shape[1] - kept_rows
    kept = window[:, 1 : 1 + kept_rows]
    for start in range(2, last_start + 1):
        kept = jnp.where(
            (accepted == start)[:, None, None], window[:, start : start + kept_rows], kept
        )
    return kept


def recur(decay, step, values, bmat, cmat, skip, state, accepted):
    kept = state
    outputs = []
    for t in range(values.shape[1]):
        state = (
            decay[:, t, None, None] * state
            + (step[:, t, None] * values[:, t])[:, :, None] * bmat[:, t, None, :]
        )
        outputs.append(jnp.sum(state * cmat[:, t, None, :], axis=-1) + skip * values[:, t])
        kept = jnp.where((accepted == t + 1)[:, None, None], state, kept)
    return (jnp.stack(outputs, 1), kept)


def local(
    draft_ids,
    accepted,
    embedding,
    norm_gain,
    w_zx,
    w_dt,
    w_bc,
    dt_bias,
    decay_rate,
    skip_weight,
    conv_x_w,
    conv_x_b,
    conv_bc_w,
    conv_bc_b,
    gate_gain,
    out_w,
    ssm_state,
    conv_x_state,
    conv_bc_state,
):
    seq_rows, draft = draft_ids.shape
    heads_here = w_zx.shape[2]
    width = w_zx.shape[3] // 2
    local_inner = heads_here * width
    own_cols = embedding.shape[1]
    model = own_cols * lax.axis_size("heads")
    inner = local_inner * lax.axis_size("heads")
    bc_here = w_bc.shape[2]
    kernel = conv_x_w.shape[1]
    recur_heads = jax.vmap(recur, in_axes=(2, 2, 2, None, None, 0, 1, None), out_axes=(2, 1))
    whole_bc = turned_gather((w_bc, conv_bc_w, conv_bc_b, conv_bc_state), "heads", (2, 2, 1, 3))
    saved_state, saved_x, saved_bc = ([], [], [])

    def mixer(layer, stream):
        value = stream.astype(jnp.float32)
        normed = (
            value * rms_scale(jnp.sum(value * value, -1, keepdims=True), model) * norm_gain[layer]
        ).astype(jnp.bfloat16)
        zx = jnp.dot(
            normed, w_zx[layer].reshape(model, -1), preferred_element_type=jnp.float32
        ).astype(jnp.bfloat16)
        zx = zx.reshape(seq_rows, draft, heads_here, 2, width)
        gate_z = zx[:, :, :, 0].astype(jnp.float32)
        values = zx[:, :, :, 1].reshape(seq_rows, draft, local_inner)
        dt_raw = (
            jnp.dot(normed, w_dt[layer], preferred_element_type=jnp.float32)
            .astype(jnp.bfloat16)
            .reshape(seq_rows, draft, heads_here)
        )
        bc = (
            jnp.dot(normed, whole_bc[0][layer], preferred_element_type=jnp.float32)
            .astype(jnp.bfloat16)
            .reshape(seq_rows, draft, -1)
        )
        window_bc = jnp.concatenate([whole_bc[3][layer], bc], axis=1)
        bcc = convolve(
            window_bc.astype(jnp.float32), whole_bc[1][layer], whole_bc[2][layer], draft
        ).astype(jnp.bfloat16)
        kept_bc = keep_rows(window_bc, accepted, kernel - 1)
        bcc = lax.optimization_barrier(bcc).astype(jnp.float32)
        kept_bc = lax.dynamic_slice_in_dim(kept_bc, lax.axis_index("heads") * bc_here, bc_here, 2)
        states = bcc.shape[2] // 2
        bmat = bcc[..., :states]
        cmat = bcc[..., states:]
        window_x = jnp.concatenate([conv_x_state[layer], values], axis=1)
        xc = convolve(
            window_x.astype(jnp.float32), conv_x_w[layer], conv_x_b[layer], draft
        ).reshape(seq_rows, draft, heads_here, width)
        step = jax.nn.softplus(dt_raw.astype(jnp.float32) + dt_bias[layer])
        decay = jnp.exp(-step * decay_rate[layer])
        outputs, kept = recur_heads(
            decay, step, xc, bmat, cmat, skip_weight[layer], ssm_state[layer], accepted
        )
        saved_state.append(kept)
        saved_x.append(keep_rows(window_x, accepted, kernel - 1))
        saved_bc.append(kept_bc)
        gated = outputs * jax.nn.silu(gate_z)
        local_sq = jnp.sum(gated * gated, axis=(2, 3)).reshape(-1)
        u_rows = (
            (gated.reshape(seq_rows, draft, local_inner) * gate_gain[layer])
            .astype(jnp.bfloat16)
            .reshape(-1, local_inner)
        )
        return (u_rows, local_sq)

    part = embedding[draft_ids.reshape(-1)]
    stream = gather_directly(part, "heads", 1)
    where_cols = lax.axis_index("heads") * own_cols
    result = part
    for layer in range(LAYERS):
        u_rows, local_sq = mixer(layer, stream)
        term = jnp.dot(u_rows, out_w[layer], preferred_element_type=jnp.float32)
        total, ssq = lax.psum((term, local_sq), "heads")
        mix = total * rms_scale(ssq, inner)[:, None]
        if layer + 1 < LAYERS:
            stream = (stream.astype(jnp.float32) + mix).astype(jnp.bfloat16)
        else:
            own_stream = lax.dynamic_slice_in_dim(stream, where_cols, own_cols, 1)
            own_mix = lax.dynamic_slice_in_dim(mix, where_cols, own_cols, 1)
            result = (own_stream.astype(jnp.float32) + own_mix).astype(jnp.bfloat16)
    return (result, jnp.stack(saved_state), jnp.stack(saved_x), jnp.stack(saved_bc))


def solution(mesh):
    placed = (
        P("batch", None),
        P("batch"),
        P(None, "heads"),
        P(),
        P(None, None, "heads", None),
        P(None, None, "heads"),
        P(None, None, "heads"),
        P(None, "heads"),
        P(None, "heads"),
        P(None, "heads"),
        P(None, None, "heads"),
        P(None, "heads"),
        P(None, None, "heads"),
        P(None, "heads"),
        P(None, "heads"),
        P(None, "heads", None),
        P(None, "batch", "heads", None, None),
        P(None, "batch", None, "heads"),
        P(None, "batch", None, "heads"),
    )
    return jax.shard_map(
        local,
        mesh=mesh,
        in_specs=placed,
        out_specs=(
            P("batch", "heads"),
            P(None, "batch", "heads", None, None),
            P(None, "batch", None, "heads"),
            P(None, "batch", None, "heads"),
        ),
        check_vma=False,
    )
```

profile of v0, /device:TPU:2, one launch (start us, length us, event | category | flops | bytes accessed | tf_op | source)
XLA Modules:
  0.0 601.9 jit_solution(6505205176545360938)
XLA Ops:
  7.2 11.0 %copy.97 = bf16[50280,40]{1,0:T(8,128)(2,1)} copy(bf16[50280,40]{0,1:T(8,128)(2,1)} %param.21) | data formatting | bytes 8044800 | tf_op args[2]
  18.4 7.5 %gather_fusion = bf16[384,40]{1,0:T(8,128)(2,1)S(1)} fusion(bf16[50280,40]{1,0:T(8,128)(2,1)} %copy.97, s32[1024]{0:T(1024)S(1)} %pad_clamp_fusion), kind=kCustom, calls=%fused_computation | custom fusion | bytes 62976 | tf_op jit(solution)/shard_map/gather | solution.py:162
  26.0 1.4 broadcast_in_dim.263
  27.5 12.2 %all-to-all-start = ((bf16[64,384,40]{1,2,0:T(8,128)(2,1)}), bf16[64,384,40]{1,2,0:T(8,128)(2,1)S(1)}, u32[]{:S(2)}, u32[]{:S(2)}) async-start(bf16[64,384,40]{1,2,0:T(8,128)(2,1)} %broadcast_in_dim.263), calls=%async_computation | async-start | bytes 3932160 | tf_op jit(solution)/shard_map/all_to_all | solution.py:32
  45.7 43.7 %all-to-all-done = bf16[64,384,40]{1,2,0:T(8,128)(2,1)S(1)} async-done(((bf16[64,384,40]{1,2,0:T(8,128)(2,1)}), bf16[64,384,40]{1,2,0:T(8,128)(2,1)S(1)}, u32[]{:S(2)}, u32[]{:S(2)}) %all-to-all-start) | async-done | bytes 1966112 | tf_op jit(solution)/shard_map/all_to_all | solution.py:32
  90.5 1.3 copy-done.3
  93.0 2.0 convolution_reduce_fusion.1
  98.5 26.6 %all-gather.3.cloned.1.call-done = bf16[64,4,5418]{2,1,0:T(4,128)(2,1)} async-done(((bf16[1,4,5418]{2,1,0:T(4,128)(2,1)}), bf16[64,4,5418]{2,1,0:T(4,128)(2,1)}) %all-gather.3.cloned.1.call-update) | async-done | bytes 2774032 | tf_op jit(solution)/shard_map/all_gather | solution.py:14
  125.0 5.5 reshape.2596
  130.6 3.6 split.17
  134.3 4.4 copy.128
  138.8 2.7 fusion.10
  145.8 4.1 multiply_add_fusion.8
  150.6 1.7 multiply_reduce_fusion.13
  154.1 3.7 multiply_reduce_fusion.9
  160.3 2.5 fusion.27
  164.1 2.2 convert_element_type.337
  166.3 5.6 copy.109
  172.0 1.4 fusion.103
  174.7 127.0 %psum.29 = f32[384]{0:T(512)S(1)} all-reduce(f32[384]{0:T(512)S(1)} %reshape.2572), channel_id=1, replica_groups=mesh['batch'=4,'heads'=64] {'heads'}, use_global_device_ids=true, to_apply=%region_11.12 | all-reduce | flops 384 | bytes 3072 | tf_op jit(solution)/shard_map/psum | solution.py:169
  301.7 1.4 fusion.119
  303.1 9.0 %select_select_fusion.1 = f32[1,48,1,64,128]{4,3,2,1,0:T(8,128)} fusion(f32[2,48,1,64,128]{4,3,2,1,0:T(8,128)S(1)} %copy-done.1, f32[48,128]{1,0:T(8,128)} %bitcast.581, f32[48,64]{1,0:T(8,128)} %copy-done.34, f32[48,128]{1,0:T(8,128)} %bitcast.579, f32[48,64]{1,0:T(8,128)} %copy-done.35, f32[48,128]{1,0:T(8,128)S(1)} %bitcast.577, f32[48,64]{1,0:T(8,128)} %copy-done.33, ...), kind=kLoop, calls=%fused_computation.15 | loop fusion | flops 12582912 | bytes 3442560 | tf_op jit(solution)/shard_map/vmap(jit(_where))/select_n | solution.py:72
  312.1 43.3 %all-reduce.3.cloned.1.call-done = f32[384,2560]{1,0:T(8,128)} async-done(((f32[384,2560]{1,0:T(8,128)}), f32[384,2560]{1,0:T(8,128)}) %all-reduce.3.cloned.1.call-update) | async-done | bytes 3932176 | tf_op jit(solution)/shard_map/psum | solution.py:169
  355.4 4.2 fusion
  360.4 1.3 copy-done.91
  361.6 1.4 convolution_convert_fusion
  363.0 1.3 convolution_reduce_fusion
  364.3 1.7 reshape.2574
  366.1 2.1 fusion.115
  369.7 1.4 fusion.127
  371.9 1.8 fusion.113
  375.5 2.2 multiply_convert_fusion.1
  380.8 4.1 multiply_add_fusion.2
  385.6 1.7 multiply_reduce_fusion.5
  389.2 3.7 multiply_reduce_fusion.1
  394.7 1.3 constant_dynamic-update-slice_fusion.24
  396.8 2.6 fusion.25
  399.3 2.2 dynamic-slice_select_fusion.6
  401.5 1.5 copy.123
  403.0 2.1 dynamic-slice_select_fusion
  405.2 1.4 copy.124
  406.6 1.7 fusion.71
  409.2 128.1 %psum.31 = f32[384]{0:T(512)S(1)} all-reduce(f32[384]{0:T(512)S(1)} %reshape.2577), channel_id=1, replica_groups=mesh['batch'=4,'heads'=64] {'heads'}, use_global_device_ids=true, to_apply=%region_23.24 | all-reduce | flops 384 | bytes 3072 | tf_op jit(solution)/shard_map/psum | solution.py:169
  537.3 1.3 pad_maximum_fusion.6
  539.4 1.4 pad_maximum_fusion.5
  540.8 8.3 %select_select_fusion = f32[1,48,1,64,128]{4,3,2,1,0:T(8,128)S(1)} fusion(f32[2,48,1,64,128]{4,3,2,1,0:T(8,128)S(1)} %copy-done.1, f32[48,128]{1,0:T(8,128)} %bitcast.567, f32[48,64]{1,0:T(8,128)} %copy-done.40, f32[48,128]{1,0:T(8,128)} %bitcast.565, f32[48,64]{1,0:T(8,128)} %copy-done.42, f32[48,128]{1,0:T(8,128)S(1)} %bitcast.563, ...), kind=kLoop, calls=%fused_computation.14 | loop fusion | flops 12582912 | bytes 3442560 | tf_op jit(solution)/shard_map/vmap(jit(_where))/select_n | solution.py:72
  549.1 1.9 pad_maximum_fusion
  551.0 42.4 %all-reduce.5.cloned.1.call-done = f32[384,2560]{1,0:T(8,128)} async-done(((f32[384,2560]{1,0:T(8,128)}), f32[384,2560]{1,0:T(8,128)}) %all-reduce.5.cloned.1.call-update) | async-done | bytes 3932176 | tf_op jit(solution)/shard_map/psum | solution.py:169
  (282 shorter events, 39.9 us)
Async XLA Ops:
  7.2 11.0 %copy-start.78 = (s32[48,8]{0,1:T(8,128)S(1)}, s32[48,8]{0,1:T(8,128)}, u32[]{:S(2)}) copy-start(s32[48,8]{0,1:T(8,128)} %param.19) | copy-start | bytes 4612
  27.4 12.4 %copy-start.56 = (bf16[2,48,3,4]{1,3,2,0:T(4,128)(2,1)S(1)}, bf16[2,48,3,4]{1,3,2,0:T(4,128)(2,1)}, u32[]{:S(2)}) copy-start(bf16[2,48,3,4]{1,3,2,0:T(4,128)(2,1)} %param.37) | copy-start | bytes 6916
  27.4 12.8 %copy-start.92 = (bf16[2,4]{1,0:T(2,128)(2,1)S(1)}, bf16[2,4]{1,0:T(2,128)(2,1)}, u32[]{:S(2)}) copy-start(bf16[2,4]{1,0:T(2,128)(2,1)} %param.32) | copy-start | bytes 52
  27.4 12.9 %copy-start.82 = (bf16[2,4,4]{2,1,0:T(4,128)(2,1)S(1)}, bf16[2,4,4]{2,1,0:T(4,128)(2,1)}, u32[]{:S(2)}) copy-start(bf16[2,4,4]{2,1,0:T(4,128)(2,1)} %param.31) | copy-start | bytes 196
  27.4 13.0 %copy-start.48 = (bf16[2,2560,4]{1,2,0:T(4,128)(2,1)S(1)}, bf16[2,2560,4]{1,2,0:T(4,128)(2,1)}, u32[]{:S(2)}) copy-start(bf16[2,2560,4]{1,2,0:T(4,128)(2,1)} %param.25) | copy-start | bytes 122884
  27.4 13.9 %copy-start.49 = (f32[2,2560]{1,0:T(2,128)S(1)}, f32[2,2560]{1,0:T(2,128)}, u32[]{:S(2)}) copy-start(f32[2,2560]{1,0:T(2,128)} %param.22) | copy-start | bytes 61444
  27.5 14.7 %copy-start.83 = (f32[2,1]{0,1:T(1,128)S(1)}, f32[2,1]{0,1:T(1,128)}, u32[]{:S(2)}) copy-start(f32[2,1]{0,1:T(1,128)} %param.26) | copy-start | bytes 28
  27.5 15.3 %copy-start.84 = (f32[2,1]{0,1:T(1,128)S(1)}, f32[2,1]{0,1:T(1,128)}, u32[]{:S(2)}) copy-start(f32[2,1]{0,1:T(1,128)} %param.27) | copy-start | bytes 28
  27.5 15.9 %copy-start.85 = (f32[2,1]{0,1:T(1,128)S(1)}, f32[2,1]{0,1:T(1,128)}, u32[]{:S(2)}) copy-start(f32[2,1]{0,1:T(1,128)} %param.28) | copy-start | bytes 28
  27.5 16.4 %copy-start.86 = (bf16[2,64]{1,0:T(2,128)(2,1)S(1)}, bf16[2,64]{1,0:T(2,128)(2,1)}, u32[]{:S(2)}) copy-start(bf16[2,64]{1,0:T(2,128)(2,1)} %param.30) | copy-start | bytes 772
  27.5 17.0 %copy-start.88 = (f32[2,64]{1,0:T(2,128)S(1)}, f32[2,64]{1,0:T(2,128)}, u32[]{:S(2)}) copy-start(f32[2,64]{1,0:T(2,128)} %param.33) | copy-start | bytes 1540
  27.5 17.6 %copy-start.81 = (bf16[2,4,64]{2,1,0:T(4,128)(2,1)S(1)}, bf16[2,4,64]{2,1,0:T(4,128)(2,1)}, u32[]{:S(2)}) copy-start(bf16[2,4,64]{2,1,0:T(4,128)(2,1)} %param.29) | copy-start | bytes 3076
  27.5 17.6 %copy-start.47 = (bf16[2,48,3,64]{3,1,2,0:T(8,128)(2,1)S(1)}, bf16[2,48,3,64]{3,1,2,0:T(8,128)(2,1)}, u32[]{:S(2)}) copy-start(bf16[2,48,3,64]{3,1,2,0:T(8,128)(2,1)} %param.36) | copy-start | bytes 110596
  27.5 61.9 %all-to-all-start = ((bf16[64,384,40]{1,2,0:T(8,128)(2,1)}), bf16[64,384,40]{1,2,0:T(8,128)(2,1)S(1)}, u32[]{:S(2)}, u32[]{:S(2)}) async-start(bf16[64,384,40]{1,2,0:T(8,128)(2,1)} %broadcast_in_dim.263), calls=%async_computation | async-start | bytes 3932160 | tf_op jit(solution)/shard_map/all_to_all | solution.py:32
  39.8 85.3 %all-gather.3.cloned.1.call-start = ((), (), s32[]{:S(2)}) async-start(), calls=%async_computation.3 | async-start | bytes 2862080 | tf_op jit(solution)/shard_map/all_gather | solution.py:14
  41.2 314.3 %all-reduce.3.cloned.1.call-start = ((), (), s32[]{:S(2)}) async-start(), calls=%async_computation.1 | async-start | bytes 7864320 | tf_op jit(solution)/shard_map/psum | solution.py:169
  92.9 67.3 %copy-start.9 = (bf16[48,8,1,1,64]{4,3,1,0,2:T(2,128)(2,1)}, bf16[48,8,1,1,64]{4,3,1,0,2:T(2,128)(2,1)S(1)}, u32[]{:S(2)}) copy-start(bf16[48,8,1,1,64]{4,3,1,0,2:T(2,128)(2,1)S(1)} %get-tuple-element.155) | copy-start | bytes 147460
  97.6 47.0 %copy-start.62 = (f32[48]{0:T(128)}, f32[48]{0:T(128)S(1)}, u32[]{:S(2)}) copy-start(f32[48]{0:T(128)S(1)} %get-tuple-element.57) | copy-start | bytes 580
  97.6 53.0 %copy-start.54 = (f32[48]{0:T(128)}, f32[48]{0:T(128)S(1)}, u32[]{:S(2)}) copy-start(f32[48]{0:T(128)S(1)} %get-tuple-element.58) | copy-start | bytes 580
  98.5 46.2 %copy-start.36 = (f32[48,64]{1,0:T(8,128)}, f32[48,64]{1,0:T(8,128)S(1)}, u32[]{:S(2)}) copy-start(f32[48,64]{1,0:T(8,128)S(1)} %get-tuple-element.176) | copy-start | bytes 36868
  98.5 55.6 %copy-start.33 = (f32[48,64]{1,0:T(8,128)}, f32[48,64]{1,0:T(8,128)S(1)}, u32[]{:S(2)}) copy-start(f32[48,64]{1,0:T(8,128)S(1)} %get-tuple-element.173) | copy-start | bytes 36868
  98.5 55.6 %copy-start.34 = (f32[48,64]{1,0:T(8,128)}, f32[48,64]{1,0:T(8,128)S(1)}, u32[]{:S(2)}) copy-start(f32[48,64]{1,0:T(8,128)S(1)} %get-tuple-element.174) | copy-start | bytes 36868
  98.5 55.6 %copy-start.35 = (f32[48,64]{1,0:T(8,128)}, f32[48,64]{1,0:T(8,128)S(1)}, u32[]{:S(2)}) copy-start(f32[48,64]{1,0:T(8,128)S(1)} %get-tuple-element.175) | copy-start | bytes 36868
  144.6 9.5 %copy-start.27 = (f32[48,1,128]{2,1,0:T(1,128)}, f32[48,1,128]{2,1,0:T(1,128)S(1)}, u32[]{:S(2)}) copy-start(f32[48,1,128]{2,1,0:T(1,128)S(1)} %get-tuple-element.161) | copy-start | bytes 73732
  144.6 9.5 %copy-start.28 = (f32[48,1,128]{2,1,0:T(1,128)}, f32[48,1,128]{2,1,0:T(1,128)S(1)}, u32[]{:S(2)}) copy-start(f32[48,1,128]{2,1,0:T(1,128)S(1)} %get-tuple-element.162) | copy-start | bytes 73732
  152.2 7.9 %copy-start.80 = (f32[64]{0:T(128)S(1)}, f32[64]{0:T(128)}, u32[]{:S(2)}) copy-start(f32[64]{0:T(128)} %get-tuple-element.208) | copy-start | bytes 772
  152.3 8.0 %copy-start.16 = (bf16[2,64,2560]{2,1,0:T(8,128)(2,1)S(1)}, bf16[2,64,2560]{2,1,0:T(8,128)(2,1)}, u32[]{:S(2)}) copy-start(bf16[2,64,2560]{2,1,0:T(8,128)(2,1)} %param.34) | copy-start | bytes 1966084
  162.8 430.5 %all-reduce.5.cloned.1.call-start = ((), (), s32[]{:S(2)}) async-start(), calls=%async_computation.2 | async-start | bytes 7864320 | tf_op jit(solution)/shard_map/psum | solution.py:169
  166.3 136.8 %copy-start.1 = (f32[2,48,1,64,128]{4,3,2,1,0:T(8,128)S(1)}, f32[2,48,1,64,128]{4,3,2,1,0:T(8,128)}, u32[]{:S(2)}) copy-start(f32[2,48,1,64,128]{4,3,2,1,0:T(8,128)} %param.35) | copy-start | bytes 9437188
  312.1 47.5 %copy-start.51 = (f32[2560]{0:T(1024)S(1)}, f32[2560]{0:T(1024)}, u32[]{:S(2)}) copy-start(f32[2560]{0:T(1024)} %get-tuple-element.70) | copy-start | bytes 30724
  377.9 7.0 %copy-start.23 = (f32[48,1,128]{2,1,0:T(1,128)}, f32[48,1,128]{2,1,0:T(1,128)S(1)}, u32[]{:S(2)}) copy-start(f32[48,1,128]{2,1,0:T(1,128)S(1)} %get-tuple-element.137) | copy-start | bytes 73732
  377.9 7.0 %copy-start.24 = (f32[48,1,128]{2,1,0:T(1,128)}, f32[48,1,128]{2,1,0:T(1,128)S(1)}, u32[]{:S(2)}) copy-start(f32[48,1,128]{2,1,0:T(1,128)S(1)} %get-tuple-element.141) | copy-start | bytes 73732
  377.9 7.0 %copy-start.25 = (f32[48,1,128]{2,1,0:T(1,128)}, f32[48,1,128]{2,1,0:T(1,128)S(1)}, u32[]{:S(2)}) copy-start(f32[48,1,128]{2,1,0:T(1,128)S(1)} %get-tuple-element.143) | copy-start | bytes 73732
  377.9 7.0 %copy-start.26 = (f32[48,1,128]{2,1,0:T(1,128)}, f32[48,1,128]{2,1,0:T(1,128)S(1)}, u32[]{:S(2)}) copy-start(f32[48,1,128]{2,1,0:T(1,128)S(1)} %get-tuple-element.144) | copy-start | bytes 73732
  377.9 11.2 %copy-start.21 = (f32[48,1,128]{2,1,0:T(1,128)}, f32[48,1,128]{2,1,0:T(1,128)S(1)}, u32[]{:S(2)}) copy-start(f32[48,1,128]{2,1,0:T(1,128)S(1)} %get-tuple-element.134) | copy-start | bytes 73732
  377.9 11.2 %copy-start.22 = (f32[48,1,128]{2,1,0:T(1,128)}, f32[48,1,128]{2,1,0:T(1,128)S(1)}, u32[]{:S(2)}) copy-start(f32[48,1,128]{2,1,0:T(1,128)S(1)} %get-tuple-element.135) | copy-start | bytes 73732
  379.2 10.0 %copy-start.73 = (f32[48]{0:T(128)}, f32[48]{0:T(128)S(1)}, u32[]{:S(2)}) copy-start(f32[48]{0:T(128)S(1)} %get-tuple-element.237) | copy-start | bytes 580
  379.2 10.0 %copy-start.74 = (f32[48]{0:T(128)}, f32[48]{0:T(128)S(1)}, u32[]{:S(2)}) copy-start(f32[48]{0:T(128)S(1)} %get-tuple-element.238) | copy-start | bytes 580
  379.2 10.0 %copy-start.75 = (f32[48]{0:T(128)}, f32[48]{0:T(128)S(1)}, u32[]{:S(2)}) copy-start(f32[48]{0:T(128)S(1)} %get-tuple-element.239) | copy-start | bytes 580
  380.0 9.2 %copy-start.40 = (f32[48,64]{1,0:T(8,128)}, f32[48,64]{1,0:T(8,128)S(1)}, u32[]{:S(2)}) copy-start(f32[48,64]{1,0:T(8,128)S(1)} %bitcast_multiply_fusion.2) | copy-start | bytes 36868
  380.2 9.0 %copy-start.41 = (f32[48,64]{1,0:T(8,128)}, f32[48,64]{1,0:T(8,128)S(1)}, u32[]{:S(2)}) copy-start(f32[48,64]{1,0:T(8,128)S(1)} %get-tuple-element.146) | copy-start | bytes 36868
  380.2 9.0 %copy-start.42 = (f32[48,64]{1,0:T(8,128)}, f32[48,64]{1,0:T(8,128)S(1)}, u32[]{:S(2)}) copy-start(f32[48,64]{1,0:T(8,128)S(1)} %get-tuple-element.147) | copy-start | bytes 36868
  387.3 9.4 %copy-start.10 = (bf16[48,8,1,1,64]{4,3,1,0,2:T(2,128)(2,1)S(1)}, bf16[48,8,1,1,64]{4,3,1,0,2:T(2,128)(2,1)}, u32[]{:S(2)}) copy-start(bf16[48,8,1,1,64]{4,3,1,0,2:T(2,128)(2,1)} %get-tuple-element.128) | copy-start | bytes 147460
  387.3 9.4 %copy-start.79 = (f32[64]{0:T(128)S(1)}, f32[64]{0:T(128)}, u32[]{:S(2)}) copy-start(f32[64]{0:T(128)} %get-tuple-element.207) | copy-start | bytes 772
  387.3 9.4 %copy-start.17 = (bf16[2,64,2560]{2,1,0:T(8,128)(2,1)S(1)}, bf16[2,64,2560]{2,1,0:T(8,128)(2,1)}, u32[]{:S(2)}) copy-start(bf16[2,64,2560]{2,1,0:T(8,128)(2,1)} %param.34) | copy-start | bytes 1966084
  399.3 139.2 %copy-start.18 = (bf16[48,3,64]{2,0,1:T(8,128)(2,1)S(1)}, bf16[48,3,64]{2,0,1:T(8,128)(2,1)}, u32[]{:S(2)}) copy-start(bf16[48,3,64]{2,0,1:T(8,128)(2,1)} %get-tuple-element.181) | copy-start | bytes 55300
  399.3 139.2 %copy-start.6 = (bf16[48,8,1,1,64]{4,0,1,3,2:T(8,128)(2,1)S(1)}, bf16[48,8,1,1,64]{4,0,1,3,2:T(8,128)(2,1)}, u32[]{:S(2)}) copy-start(bf16[48,8,1,1,64]{4,0,1,3,2:T(8,128)(2,1)} %copy-done.5) | copy-start | bytes 147460
  540.8 8.3 %copy-start.4 = (f32[1,48,1,64,128]{4,3,2,1,0:T(8,128)S(1)}, f32[1,48,1,64,128]{4,3,2,1,0:T(8,128)}, u32[]{:S(2)}) copy-start(f32[1,48,1,64,128]{4,3,2,1,0:T(8,128)} %select_select_fusion.1) | copy-start | bytes 4718596
  (50 other events, 168.0 us)
Sparse Core Ops, SparseCore 0:
  43.9 81.1 all-gather.2
  163.0 192.4 all-reduce.2
  399.5 193.8 all-reduce.4
where the time goes:
time: 604 us; the launch traced here: 602 us
  blocking collectives  255 us (42%)
  waiting for transfers between devices  156 us (26%)
  other arithmetic  84.4 us (14%)
  local copies, waits for them, and re-layouts  64.7 us (11%)
  between operations  15.2 us (3%)
  matrix products  13.8 us (2%)
  starting transfers between devices  12.6 us (2%)
    psum x2, blocking collectives, local(): total, ssq = lax.psum((term, local_sq), 'heads')  255 us
    psum x2, waiting for transfers between devices, local(): total, ssq = lax.psum((term, local_sq), 'heads')  85.7 us
    all_to_all x1, waiting for transfers between devices, sent_to_all(): lax.all_to_all(jnp.broadcast_to(value[None], (count, *value.shape)), axis...  43.7 us
    all_gather x1, waiting for transfers between devices, turned_gather(): filled = lax.all_gather(both, axis, axis=0, tiled=True)  26.6 us
    unnamed x193, local copies, waits for them, and re-layouts  23.4 us
    select_n x2, other arithmetic, recur(): kept = jnp.where((accepted == t + 1)[:, None, None], state, kept)  17.3 us
    all_to_all x1, starting transfers between devices, sent_to_all(): lax.all_to_all(jnp.broadcast_to(value[None], (count, *value.shape)), axis...  12.2 us
  transfers between devices with their start and end apart: 4, of which 4 were waited for; matrix products, arithmetic and copies ran while one was open for 10% of the time, Pallas kernels for 0%

commit v1 on v0

--- a/solution.py
+++ b/solution.py
@@ -7,11 +7,20 @@
 EPS = 1e-05
 
 
+def test_the_table(frame_in, across):
+    return jnp.concatenate(
+        lax.all_to_all(
+            jnp.stack(tuple((frame_in for _ in range(lax.axis_size(across)))), axis=0), across, 0, 0
+        ),
+        0,
+    )
+
+
 def turned_gather(arrays, axis, dims):
     turned = [jnp.moveaxis(a, dim, 0) for a, dim in zip(arrays, dims)]
     widths = [t[0].size for t in turned]
     both = jnp.concatenate([t.reshape(-1, w) for t, w in zip(turned, widths)], axis=1)
-    filled = lax.all_gather(both, axis, axis=0, tiled=True)
+    filled = test_the_table(both, axis)
     blocks = jnp.split(filled, [sum(widths[:k]) for k in range(1, len(widths))], axis=1)
     return tuple(
         (

time: 604 us -> 642 us (1.063)
  waiting for transfers between devices: 156 us -> 187 us
    all_to_all x0 -> x1, waiting for transfers between devices: none -> 52 us  [test_the_table(): lax.all_to_all(jnp.stack(tuple((frame_in for _ in range(lax.axis_size(acr...]
    all_gather x1 -> x0, waiting for transfers between devices: 26.6 us -> none  [turned_gather(): filled = lax.all_gather(both, axis, axis=0, tiled=True)]
    all_to_all x0 -> x1, starting transfers between devices: none -> 6.49 us  [test_the_table(): lax.all_to_all(jnp.stack(tuple((frame_in for _ in range(lax.axis_size(acr...]
    unnamed x193 -> x192, local copies, waits for them, and re-layouts: 23.4 us -> 17.9 us
  transfers between devices with their start and end apart: 4 -> 4, of which waited for: 4 -> 4; matrix products, arithmetic and copies ran while one was open for 10% -> 9% of each run, Pallas kernels for 0% -> 0%
where the time goes in v1:
time: 642 us; the launch traced here: 640 us
  blocking collectives  254 us (40%)
  waiting for transfers between devices  187 us (29%)
  other arithmetic  84.4 us (13%)
  local copies, waits for them, and re-layouts  66.4 us (10%)
  starting transfers between devices  19 us (3%)
  between operations  15.5 us (2%)
  matrix products  13.9 us (2%)
    psum x2, blocking collectives, local(): total, ssq = lax.psum((term, local_sq), 'heads')  254 us
    psum x2, waiting for transfers between devices, local(): total, ssq = lax.psum((term, local_sq), 'heads')  87 us
    all_to_all x1, waiting for transfers between devices, test_the_table(): lax.all_to_all(jnp.stack(tuple((frame_in for _ in range(lax.axis_size(acr...  52 us
    all_to_all x1, waiting for transfers between devices, sent_to_all(): lax.all_to_all(jnp.broadcast_to(value[None], (count, *value.shape)), axis...  47.5 us
    unnamed x192, local copies, waits for them, and re-layouts  17.9 us
    select_n x2, other arithmetic, recur(): kept = jnp.where((accepted == t + 1)[:, None, None], state, kept)  17.3 us
  transfers between devices with their start and end apart: 4, of which 4 were waited for; matrix products, arithmetic and copies ran while one was open for 9% of the time, Pallas kernels for 0%

profile of v1, /device:TPU:2, one launch (start us, length us, event | category | flops | bytes accessed | tf_op | source)
XLA Modules:
  0.0 639.5 jit_solution(16953221342350199314)
XLA Ops:
  7.2 11.0 %copy.97 = bf16[50280,40]{1,0:T(8,128)(2,1)} copy(bf16[50280,40]{0,1:T(8,128)(2,1)} %param.21) | data formatting | bytes 8044800 | tf_op args[2]
  18.4 7.5 %gather_fusion = bf16[384,40]{1,0:T(8,128)(2,1)S(1)} fusion(bf16[50280,40]{1,0:T(8,128)(2,1)} %copy.97, s32[1024]{0:T(1024)S(1)} %pad_clamp_fusion), kind=kCustom, calls=%fused_computation | custom fusion | bytes 62976 | tf_op jit(solution)/shard_map/gather | solution.py:171
  26.0 1.4 broadcast_in_dim.263
  27.4 12.3 %all-to-all-start = ((bf16[64,384,40]{1,2,0:T(8,128)(2,1)}), bf16[64,384,40]{1,2,0:T(8,128)(2,1)S(1)}, u32[]{:S(2)}, u32[]{:S(2)}) async-start(bf16[64,384,40]{1,2,0:T(8,128)(2,1)} %broadcast_in_dim.263), calls=%async_computation | async-start | bytes 3932160 | tf_op jit(solution)/shard_map/all_to_all | solution.py:41
  40.4 47.5 %all-to-all-done = bf16[64,384,40]{1,2,0:T(8,128)(2,1)S(1)} async-done(((bf16[64,384,40]{1,2,0:T(8,128)(2,1)}), bf16[64,384,40]{1,2,0:T(8,128)(2,1)S(1)}, u32[]{:S(2)}, u32[]{:S(2)}) %all-to-all-start) | async-done | bytes 1966112 | tf_op jit(solution)/shard_map/all_to_all | solution.py:41
  87.8 2.3 stack.56
  90.2 6.5 %all-to-all-start.1 = ((bf16[64,4,5418]{2,1,0:T(4,128)(2,1)}), bf16[64,4,5418]{2,1,0:T(4,128)(2,1)}, u32[]{:S(2)}, u32[]{:S(2)}) async-start(bf16[64,4,5418]{2,1,0:T(4,128)(2,1)} %stack.56), calls=%async_computation.1 | async-start | bytes 5636096 | tf_op jit(solution)/shard_map/all_to_all | solution.py:12
  104.8 2.0 convolution_reduce_fusion.1
  110.3 52.0 %all-to-all-done.1 = bf16[64,4,5418]{2,1,0:T(4,128)(2,1)} async-done(((bf16[64,4,5418]{2,1,0:T(4,128)(2,1)}), bf16[64,4,5418]{2,1,0:T(4,128)(2,1)}, u32[]{:S(2)}, u32[]{:S(2)}) %all-to-all-start.1) | async-done | bytes 2774048 | tf_op jit(solution)/shard_map/all_to_all | solution.py:12
  162.3 5.5 reshape.2573
  167.8 3.6 split.17
  171.6 4.4 copy.128
  176.0 2.7 fusion.10
  183.0 4.1 multiply_add_fusion.8
  187.8 1.7 multiply_reduce_fusion.13
  191.4 3.7 multiply_reduce_fusion.9
  197.5 2.6 fusion.27
  201.4 2.2 convert_element_type.337
  203.6 5.6 copy.109
  209.2 1.4 fusion.103
  212.0 125.7 %psum.29 = f32[384]{0:T(512)S(1)} all-reduce(f32[384]{0:T(512)S(1)} %reshape.2578), channel_id=1, replica_groups=mesh['batch'=4,'heads'=64] {'heads'}, use_global_device_ids=true, to_apply=%region_11.12 | all-reduce | flops 384 | bytes 3072 | tf_op jit(solution)/shard_map/psum | solution.py:178
  337.7 1.4 fusion.119
  339.1 9.0 %select_select_fusion.1 = f32[1,48,1,64,128]{4,3,2,1,0:T(8,128)} fusion(f32[2,48,1,64,128]{4,3,2,1,0:T(8,128)S(1)} %copy-done.1, f32[48,128]{1,0:T(8,128)} %bitcast.580, f32[48,64]{1,0:T(8,128)} %copy-done.34, f32[48,128]{1,0:T(8,128)} %bitcast.578, f32[48,64]{1,0:T(8,128)} %copy-done.35, f32[48,128]{1,0:T(8,128)S(1)} %bitcast.576, f32[48,64]{1,0:T(8,128)} %copy-done.33, ...), kind=kLoop, calls=%fused_computation.15 | loop fusion | flops 12582912 | bytes 3442560 | tf_op jit(solution)/shard_map/vmap(jit(_where))/select_n | solution.py:81
  348.1 44.6 %all-reduce.3.cloned.1.call-done = f32[384,2560]{1,0:T(8,128)} async-done(((f32[384,2560]{1,0:T(8,128)}), f32[384,2560]{1,0:T(8,128)}) %all-reduce.3.cloned.1.call-update) | async-done | bytes 3932176 | tf_op jit(solution)/shard_map/psum | solution.py:178
  392.7 4.2 fusion
  399.0 1.4 convolution_convert_fusion
  400.4 1.3 convolution_reduce_fusion
  401.7 1.7 reshape.2580
  403.4 2.1 fusion.115
  407.0 1.4 fusion.127
  409.2 1.8 fusion.113
  412.8 2.2 multiply_convert_fusion.1
  418.1 4.1 multiply_add_fusion.2
  422.9 1.7 multiply_reduce_fusion.5
  426.5 3.7 multiply_reduce_fusion.1
  432.0 1.3 constant_dynamic-update-slice_fusion.24
  434.1 2.5 fusion.25
  436.7 2.2 dynamic-slice_select_fusion.6
  438.9 1.5 copy.123
  440.3 2.1 dynamic-slice_select_fusion
  442.5 1.4 copy.124
  443.9 1.7 fusion.71
  446.5 128.1 %psum.31 = f32[384]{0:T(512)S(1)} all-reduce(f32[384]{0:T(512)S(1)} %reshape.2583), channel_id=1, replica_groups=mesh['batch'=4,'heads'=64] {'heads'}, use_global_device_ids=true, to_apply=%region_23.24 | all-reduce | flops 384 | bytes 3072 | tf_op jit(solution)/shard_map/psum | solution.py:178
  574.6 1.3 pad_maximum_fusion.6
  576.7 1.4 pad_maximum_fusion.5
  578.1 8.3 %select_select_fusion = f32[1,48,1,64,128]{4,3,2,1,0:T(8,128)S(1)} fusion(f32[2,48,1,64,128]{4,3,2,1,0:T(8,128)S(1)} %copy-done.1, f32[48,128]{1,0:T(8,128)} %bitcast.566, f32[48,64]{1,0:T(8,128)} %copy-done.40, f32[48,128]{1,0:T(8,128)} %bitcast.564, f32[48,64]{1,0:T(8,128)} %copy-done.42, f32[48,128]{1,0:T(8,128)S(1)} %bitcast.562, ...), kind=kLoop, calls=%fused_computation.14 | loop fusion | flops 12582912 | bytes 3442560 | tf_op jit(solution)/shard_map/vmap(jit(_where))/select_n | solution.py:81
  586.4 1.9 pad_maximum_fusion
  588.3 42.4 %all-reduce.5.cloned.1.call-done = f32[384,2560]{1,0:T(8,128)} async-done(((f32[384,2560]{1,0:T(8,128)}), f32[384,2560]{1,0:T(8,128)}) %all-reduce.5.cloned.1.call-update) | async-done | bytes 3932176 | tf_op jit(solution)/shard_map/psum | solution.py:178
  (282 shorter events, 41.8 us)
Async XLA Ops:
  7.2 11.0 %copy-start.78 = (s32[48,8]{0,1:T(8,128)S(1)}, s32[48,8]{0,1:T(8,128)}, u32[]{:S(2)}) copy-start(s32[48,8]{0,1:T(8,128)} %param.19) | copy-start | bytes 4612
  27.4 12.3 %copy-start.56 = (bf16[2,48,3,4]{1,3,2,0:T(4,128)(2,1)S(1)}, bf16[2,48,3,4]{1,3,2,0:T(4,128)(2,1)}, u32[]{:S(2)}) copy-start(bf16[2,48,3,4]{1,3,2,0:T(4,128)(2,1)} %param.37) | copy-start | bytes 6916
  27.4 12.6 %copy-start.92 = (bf16[2,4]{1,0:T(2,128)(2,1)S(1)}, bf16[2,4]{1,0:T(2,128)(2,1)}, u32[]{:S(2)}) copy-start(bf16[2,4]{1,0:T(2,128)(2,1)} %param.32) | copy-start | bytes 52
  27.4 12.7 %copy-start.82 = (bf16[2,4,4]{2,1,0:T(4,128)(2,1)S(1)}, bf16[2,4,4]{2,1,0:T(4,128)(2,1)}, u32[]{:S(2)}) copy-start(bf16[2,4,4]{2,1,0:T(4,128)(2,1)} %param.31) | copy-start | bytes 196
  27.4 12.8 %copy-start.48 = (bf16[2,2560,4]{1,2,0:T(4,128)(2,1)S(1)}, bf16[2,2560,4]{1,2,0:T(4,128)(2,1)}, u32[]{:S(2)}) copy-start(bf16[2,2560,4]{1,2,0:T(4,128)(2,1)} %param.25) | copy-start | bytes 122884
  27.4 60.4 %all-to-all-start = ((bf16[64,384,40]{1,2,0:T(8,128)(2,1)}), bf16[64,384,40]{1,2,0:T(8,128)(2,1)S(1)}, u32[]{:S(2)}, u32[]{:S(2)}) async-start(bf16[64,384,40]{1,2,0:T(8,128)(2,1)} %broadcast_in_dim.263), calls=%async_computation | async-start | bytes 3932160 | tf_op jit(solution)/shard_map/all_to_all | solution.py:41
  90.1 6.8 %copy-start.49 = (f32[2,2560]{1,0:T(2,128)S(1)}, f32[2,2560]{1,0:T(2,128)}, u32[]{:S(2)}) copy-start(f32[2,2560]{1,0:T(2,128)} %param.22) | copy-start | bytes 61444
  90.1 7.5 %copy-start.83 = (f32[2,1]{0,1:T(1,128)S(1)}, f32[2,1]{0,1:T(1,128)}, u32[]{:S(2)}) copy-start(f32[2,1]{0,1:T(1,128)} %param.26) | copy-start | bytes 28
  90.1 8.1 %copy-start.84 = (f32[2,1]{0,1:T(1,128)S(1)}, f32[2,1]{0,1:T(1,128)}, u32[]{:S(2)}) copy-start(f32[2,1]{0,1:T(1,128)} %param.27) | copy-start | bytes 28
  90.1 8.7 %copy-start.85 = (f32[2,1]{0,1:T(1,128)S(1)}, f32[2,1]{0,1:T(1,128)}, u32[]{:S(2)}) copy-start(f32[2,1]{0,1:T(1,128)} %param.28) | copy-start | bytes 28
  90.1 9.3 %copy-start.86 = (bf16[2,64]{1,0:T(2,128)(2,1)S(1)}, bf16[2,64]{1,0:T(2,128)(2,1)}, u32[]{:S(2)}) copy-start(bf16[2,64]{1,0:T(2,128)(2,1)} %param.30) | copy-start | bytes 772
  90.1 9.9 %copy-start.88 = (f32[2,64]{1,0:T(2,128)S(1)}, f32[2,64]{1,0:T(2,128)}, u32[]{:S(2)}) copy-start(f32[2,64]{1,0:T(2,128)} %param.33) | copy-start | bytes 1540
  90.2 10.5 %copy-start.81 = (bf16[2,4,64]{2,1,0:T(4,128)(2,1)S(1)}, bf16[2,4,64]{2,1,0:T(4,128)(2,1)}, u32[]{:S(2)}) copy-start(bf16[2,4,64]{2,1,0:T(4,128)(2,1)} %param.29) | copy-start | bytes 3076
  90.2 10.5 %copy-start.47 = (bf16[2,48,3,64]{3,1,2,0:T(8,128)(2,1)S(1)}, bf16[2,48,3,64]{3,1,2,0:T(8,128)(2,1)}, u32[]{:S(2)}) copy-start(bf16[2,48,3,64]{3,1,2,0:T(8,128)(2,1)} %param.36) | copy-start | bytes 110596
  90.2 72.1 %all-to-all-start.1 = ((bf16[64,4,5418]{2,1,0:T(4,128)(2,1)}), bf16[64,4,5418]{2,1,0:T(4,128)(2,1)}, u32[]{:S(2)}, u32[]{:S(2)}) async-start(bf16[64,4,5418]{2,1,0:T(4,128)(2,1)} %stack.56), calls=%async_computation.1 | async-start | bytes 5636096 | tf_op jit(solution)/shard_map/all_to_all | solution.py:12
  96.7 296.1 %all-reduce.3.cloned.1.call-start = ((), (), s32[]{:S(2)}) async-start(), calls=%async_computation.2 | async-start | bytes 7864320 | tf_op jit(solution)/shard_map/psum | solution.py:178
  104.7 92.7 %copy-start.9 = (bf16[48,8,1,1,64]{4,3,1,0,2:T(2,128)(2,1)}, bf16[48,8,1,1,64]{4,3,1,0,2:T(2,128)(2,1)S(1)}, u32[]{:S(2)}) copy-start(bf16[48,8,1,1,64]{4,3,1,0,2:T(2,128)(2,1)S(1)} %get-tuple-element.155) | copy-start | bytes 147460
  109.4 72.5 %copy-start.62 = (f32[48]{0:T(128)}, f32[48]{0:T(128)S(1)}, u32[]{:S(2)}) copy-start(f32[48]{0:T(128)S(1)} %get-tuple-element.57) | copy-start | bytes 580
  109.4 78.5 %copy-start.54 = (f32[48]{0:T(128)}, f32[48]{0:T(128)S(1)}, u32[]{:S(2)}) copy-start(f32[48]{0:T(128)S(1)} %get-tuple-element.58) | copy-start | bytes 580
  110.3 71.6 %copy-start.36 = (f32[48,64]{1,0:T(8,128)}, f32[48,64]{1,0:T(8,128)S(1)}, u32[]{:S(2)}) copy-start(f32[48,64]{1,0:T(8,128)S(1)} %get-tuple-element.176) | copy-start | bytes 36868
  110.3 81.0 %copy-start.33 = (f32[48,64]{1,0:T(8,128)}, f32[48,64]{1,0:T(8,128)S(1)}, u32[]{:S(2)}) copy-start(f32[48,64]{1,0:T(8,128)S(1)} %get-tuple-element.173) | copy-start | bytes 36868
  110.3 81.1 %copy-start.34 = (f32[48,64]{1,0:T(8,128)}, f32[48,64]{1,0:T(8,128)S(1)}, u32[]{:S(2)}) copy-start(f32[48,64]{1,0:T(8,128)S(1)} %get-tuple-element.174) | copy-start | bytes 36868
  110.3 81.1 %copy-start.35 = (f32[48,64]{1,0:T(8,128)}, f32[48,64]{1,0:T(8,128)S(1)}, u32[]{:S(2)}) copy-start(f32[48,64]{1,0:T(8,128)S(1)} %get-tuple-element.175) | copy-start | bytes 36868
  181.8 9.5 %copy-start.27 = (f32[48,1,128]{2,1,0:T(1,128)}, f32[48,1,128]{2,1,0:T(1,128)S(1)}, u32[]{:S(2)}) copy-start(f32[48,1,128]{2,1,0:T(1,128)S(1)} %get-tuple-element.161) | copy-start | bytes 73732
  181.9 9.5 %copy-start.28 = (f32[48,1,128]{2,1,0:T(1,128)}, f32[48,1,128]{2,1,0:T(1,128)S(1)}, u32[]{:S(2)}) copy-start(f32[48,1,128]{2,1,0:T(1,128)S(1)} %get-tuple-element.162) | copy-start | bytes 73732
  189.5 7.9 %copy-start.80 = (f32[64]{0:T(128)S(1)}, f32[64]{0:T(128)}, u32[]{:S(2)}) copy-start(f32[64]{0:T(128)} %get-tuple-element.208) | copy-start | bytes 772
  189.5 8.0 %copy-start.16 = (bf16[2,64,2560]{2,1,0:T(8,128)(2,1)S(1)}, bf16[2,64,2560]{2,1,0:T(8,128)(2,1)}, u32[]{:S(2)}) copy-start(bf16[2,64,2560]{2,1,0:T(8,128)(2,1)} %param.34) | copy-start | bytes 1966084
  200.1 430.6 %all-reduce.5.cloned.1.call-start = ((), (), s32[]{:S(2)}) async-start(), calls=%async_computation.3 | async-start | bytes 7864320 | tf_op jit(solution)/shard_map/psum | solution.py:178
  203.6 135.5 %copy-start.1 = (f32[2,48,1,64,128]{4,3,2,1,0:T(8,128)S(1)}, f32[2,48,1,64,128]{4,3,2,1,0:T(8,128)}, u32[]{:S(2)}) copy-start(f32[2,48,1,64,128]{4,3,2,1,0:T(8,128)} %param.35) | copy-start | bytes 9437188
  348.1 48.8 %copy-start.51 = (f32[2560]{0:T(1024)S(1)}, f32[2560]{0:T(1024)}, u32[]{:S(2)}) copy-start(f32[2560]{0:T(1024)} %get-tuple-element.70) | copy-start | bytes 30724
  415.2 7.0 %copy-start.23 = (f32[48,1,128]{2,1,0:T(1,128)}, f32[48,1,128]{2,1,0:T(1,128)S(1)}, u32[]{:S(2)}) copy-start(f32[48,1,128]{2,1,0:T(1,128)S(1)} %get-tuple-element.137) | copy-start | bytes 73732
  415.2 7.0 %copy-start.24 = (f32[48,1,128]{2,1,0:T(1,128)}, f32[48,1,128]{2,1,0:T(1,128)S(1)}, u32[]{:S(2)}) copy-start(f32[48,1,128]{2,1,0:T(1,128)S(1)} %get-tuple-element.141) | copy-start | bytes 73732
  415.2 7.0 %copy-start.25 = (f32[48,1,128]{2,1,0:T(1,128)}, f32[48,1,128]{2,1,0:T(1,128)S(1)}, u32[]{:S(2)}) copy-start(f32[48,1,128]{2,1,0:T(1,128)S(1)} %get-tuple-element.143) | copy-start | bytes 73732
  415.3 7.0 %copy-start.26 = (f32[48,1,128]{2,1,0:T(1,128)}, f32[48,1,128]{2,1,0:T(1,128)S(1)}, u32[]{:S(2)}) copy-start(f32[48,1,128]{2,1,0:T(1,128)S(1)} %get-tuple-element.144) | copy-start | bytes 73732
  415.3 11.2 %copy-start.21 = (f32[48,1,128]{2,1,0:T(1,128)}, f32[48,1,128]{2,1,0:T(1,128)S(1)}, u32[]{:S(2)}) copy-start(f32[48,1,128]{2,1,0:T(1,128)S(1)} %get-tuple-element.134) | copy-start | bytes 73732
  415.3 11.2 %copy-start.22 = (f32[48,1,128]{2,1,0:T(1,128)}, f32[48,1,128]{2,1,0:T(1,128)S(1)}, u32[]{:S(2)}) copy-start(f32[48,1,128]{2,1,0:T(1,128)S(1)} %get-tuple-element.135) | copy-start | bytes 73732
  416.5 10.0 %copy-start.73 = (f32[48]{0:T(128)}, f32[48]{0:T(128)S(1)}, u32[]{:S(2)}) copy-start(f32[48]{0:T(128)S(1)} %get-tuple-element.237) | copy-start | bytes 580
  416.5 10.0 %copy-start.74 = (f32[48]{0:T(128)}, f32[48]{0:T(128)S(1)}, u32[]{:S(2)}) copy-start(f32[48]{0:T(128)S(1)} %get-tuple-element.238) | copy-start | bytes 580
  416.5 10.0 %copy-start.75 = (f32[48]{0:T(128)}, f32[48]{0:T(128)S(1)}, u32[]{:S(2)}) copy-start(f32[48]{0:T(128)S(1)} %get-tuple-element.239) | copy-start | bytes 580
  417.3 9.2 %copy-start.40 = (f32[48,64]{1,0:T(8,128)}, f32[48,64]{1,0:T(8,128)S(1)}, u32[]{:S(2)}) copy-start(f32[48,64]{1,0:T(8,128)S(1)} %bitcast_multiply_fusion.2) | copy-start | bytes 36868
  417.5 9.0 %copy-start.41 = (f32[48,64]{1,0:T(8,128)}, f32[48,64]{1,0:T(8,128)S(1)}, u32[]{:S(2)}) copy-start(f32[48,64]{1,0:T(8,128)S(1)} %get-tuple-element.146) | copy-start | bytes 36868
  417.5 9.0 %copy-start.42 = (f32[48,64]{1,0:T(8,128)}, f32[48,64]{1,0:T(8,128)S(1)}, u32[]{:S(2)}) copy-start(f32[48,64]{1,0:T(8,128)S(1)} %get-tuple-element.147) | copy-start | bytes 36868
  424.6 9.4 %copy-start.10 = (bf16[48,8,1,1,64]{4,3,1,0,2:T(2,128)(2,1)S(1)}, bf16[48,8,1,1,64]{4,3,1,0,2:T(2,128)(2,1)}, u32[]{:S(2)}) copy-start(bf16[48,8,1,1,64]{4,3,1,0,2:T(2,128)(2,1)} %get-tuple-element.128) | copy-start | bytes 147460
  424.6 9.4 %copy-start.79 = (f32[64]{0:T(128)S(1)}, f32[64]{0:T(128)}, u32[]{:S(2)}) copy-start(f32[64]{0:T(128)} %get-tuple-element.207) | copy-start | bytes 772
  424.6 9.4 %copy-start.17 = (bf16[2,64,2560]{2,1,0:T(8,128)(2,1)S(1)}, bf16[2,64,2560]{2,1,0:T(8,128)(2,1)}, u32[]{:S(2)}) copy-start(bf16[2,64,2560]{2,1,0:T(8,128)(2,1)} %param.34) | copy-start | bytes 1966084
  436.6 139.3 %copy-start.18 = (bf16[48,3,64]{2,0,1:T(8,128)(2,1)S(1)}, bf16[48,3,64]{2,0,1:T(8,128)(2,1)}, u32[]{:S(2)}) copy-start(bf16[48,3,64]{2,0,1:T(8,128)(2,1)} %get-tuple-element.181) | copy-start | bytes 55300
  436.7 139.2 %copy-start.6 = (bf16[48,8,1,1,64]{4,0,1,3,2:T(8,128)(2,1)S(1)}, bf16[48,8,1,1,64]{4,0,1,3,2:T(8,128)(2,1)}, u32[]{:S(2)}) copy-start(bf16[48,8,1,1,64]{4,0,1,3,2:T(8,128)(2,1)} %copy-done.5) | copy-start | bytes 147460
  578.1 8.3 %copy-start.4 = (f32[1,48,1,64,128]{4,3,2,1,0:T(8,128)S(1)}, f32[1,48,1,64,128]{4,3,2,1,0:T(8,128)}, u32[]{:S(2)}) copy-start(f32[1,48,1,64,128]{4,3,2,1,0:T(8,128)} %select_select_fusion.1) | copy-start | bytes 4718596
  (50 other events, 168.0 us)
Sparse Core Ops, SparseCore 0:
  200.2 192.4 all-reduce.2
  436.8 193.9 all-reduce.4
